TPU v7x, 32 devices: a whole 2x2x4 slice. The times are simulated.
32 devices in a mesh: dev: 32 (over z, y, x, core).
Axes of the slice: x: 2, y: 2, z: 4, core: 2. Of those that a mesh axis runs over, the one named last changes fastest.
Arguments:
- state_real: float32 [4194304], P('dev'), may hold values from -24 to 24, as said below
- state_imag: float32 [4194304], P('dev'), may hold values from -24 to 24, as said below
- subsystem: int32 [3], replicated, may hold values from 0 to 16, as said below
Outputs:
- rho_real: float32 [256, 256], P('dev')
- rho_imag: float32 [256, 256], P('dev')
Inputs may be any that keep to these rules, and one draw needn't show every extreme that they name: `subsystem`: the 3 entries are distinct local bit positions in ascending order; the first is always 0 and the last always 17 - 1. `state_real`: real parts of amplitudes; their typical size changes between aligned blocks of 2**(11) local indices by up to a factor of 16. `state_imag`: imaginary parts of amplitudes, with the same block sizes as the real parts.
All inputs are finite; a program needn't handle non-finite values.
Results may differ from a plain program's by a relative error of at most 0.0001.
Values sent between devices are 32-bit elements; how exact they have to be, the bound alone decides.
A program may use at most 192 MiB of HBM per device.

v0:
```python
import functools

import jax
import jax.numpy as jnp
from jax import lax
from jax.experimental import pallas as pl
from jax.experimental.pallas import tpu as pltpu
from jax.sharding import PartitionSpec as P

MESH = pl.DeviceIdType.MESH


def exchange_kernel(n, sub_hbm, re_hbm, im_hbm, rows_ref, sub_ref, state, mixed, send, recv,
                    part_ref, pair_ref, load_sem, send_sem, recv_sem,
                    pair_send, pair_recv, row_send, row_recv):
    me = lax.axis_index("dev")
    barrier = pltpu.get_barrier_semaphore()

    def greet(k, carry):
        pl.semaphore_signal(
            barrier, inc=1, device_id=(jnp.bitwise_xor(me, n - k),), device_id_type=MESH
        )
        return carry

    lax.fori_loop(1, n, greet, 0)
    loads = [
        pltpu.make_async_copy(sub_hbm, sub_ref, load_sem.at[2]),
        pltpu.make_async_copy(re_hbm, state.at[0], load_sem.at[0]),
        pltpu.make_async_copy(im_hbm, state.at[1], load_sem.at[1]),
    ]
    for load in loads:
        load.start()
    vregs = state.shape[1]
    quarter = vregs // 4
    bits = vregs.bit_length() - 1
    width = vregs // n

    for load in loads:
        load.wait()

    lane = lax.broadcasted_iota(jnp.int32, (8, 128), 1)
    sub = lax.broadcasted_iota(jnp.int32, (8, 128), 0)

    mid = sub_ref[1]
    lane_step = jnp.int32(1)
    for b in range(1, 7):
        lane_step = jnp.where(mid == b, 2**b, lane_step)
    top = 10 + bits - 1
    in_lane = (mid < 7) | (mid == top - 1)
    stride = jnp.int32(vregs // 8)
    for b in range(10, top - 1):
        stride = jnp.where(mid == b, 2 ** (b - 10), stride)
    stride = jnp.where(mid == 7, vregs // 4, stride)
    stride = jnp.where(mid == 9, vregs // 2, stride)
    fixed = mid == 8
    lane_on = jnp.where(in_lane, lane_step, 0)
    lane_hit = jnp.bitwise_and(lane, lane_on) != 0
    lane_keep = lane_hit | (jnp.where(in_lane, 0, 1) != jnp.bitwise_and(lane, 0))
    sub_on = jnp.where(fixed, 0, 2)
    sub_hit = jnp.bitwise_and(sub, sub_on) != 0
    sub_keep = sub_hit | (jnp.where(fixed, 1, 0) != jnp.bitwise_and(sub, 0))

    high4 = sub >= 4
    odd_sub = jnp.bitwise_and(sub, 1) != 0
    odd_lane = jnp.bitwise_and(lane, 1) != 0

    def swap(a, b, hit, keep, step, axis):
        size = (8, 128)[axis]
        back = size - step
        return (
            jnp.where(hit, pltpu.roll(b, step, axis), a),
            jnp.where(keep, b, pltpu.roll(a, back, axis)),
        )

    def first_pass(v, carry):
        for c in range(2):
            x = [state[c, v + quarter * k] for k in range(4)]
            x[0], x[2] = swap(x[0], x[2], high4, high4, 4, 0)
            x[1], x[3] = swap(x[1], x[3], high4, high4, 4, 0)
            for k in (0, 2):
                a, b = swap(x[k], x[k + 1], odd_lane, odd_lane, 1, 1)
                x[k], x[k + 1] = swap(a, b, odd_sub, odd_sub, 1, 0)
            for k in range(4):
                mixed[c, v + quarter * k] = x[k]
        return carry

    lax.fori_loop(0, quarter, first_pass, 0, unroll=4)

    dests = max(1, 2 // width)
    pairs = max(1, width // 2)
    rounds = n // dests

    def second_pass(at, carry):
        for c in range(2):
            for p in range(pairs):
                u = at * pairs + p
                low = jnp.bitwise_and(u, stride - 1)
                first = 2 * u - low
                a = mixed[c, first]
                b = mixed[c, first + stride]
                a, b = swap(a, b, lane_hit, lane_keep, lane_step, 1)
                a, b = swap(a, b, sub_hit, sub_keep, 2, 0)
                for w, value in enumerate((a, b)):
                    dest, tile = divmod(2 * p + w, width)
                    column = (c * width + tile) * 128
                    send[at * dests + dest, :, column : column + 128] = value
        return carry

    lax.fori_loop(0, rounds, second_pass, 0, unroll=4)

    core = lax.rem(me, 2)
    other = 1 - core
    chip = me // 2
    chips = n // 2
    pl.semaphore_wait(barrier, n - 1)

    def send_chunk(k, carry):
        j = jnp.bitwise_xor(me, n - k)
        pltpu.make_async_remote_copy(
            src_ref=send.at[j], dst_ref=recv.at[chip, core], send_sem=send_sem,
            recv_sem=recv_sem, device_id=(j,), device_id_type=MESH,
        ).start()
        return carry

    lax.fori_loop(1, n, send_chunk, 0)
    pltpu.make_async_copy(send.at[me], recv.at[chip, core], recv_sem).start()
    pltpu.make_async_copy(recv, recv, recv_sem).wait()

    full = 8 * n
    depth = width * 128
    block = min(full // 2, 256)
    blocks = full // 2 // block
    group = block // 8

    def split(x):
        high = x.astype(jnp.bfloat16)
        return high, (x - high.astype(jnp.float32)).astype(jnp.bfloat16)

    def dot(x, y):
        return lax.dot_general(x, y, (((1,), (1,)), ((), ())), preferred_element_type=jnp.float32)

    right_h, right_l = split(recv[...].reshape(full, 2 * depth))

    def gram(side):
        def gram_block(i, carry):
            chunk = pl.ds(i * group, group)
            left = recv[chunk, side].reshape(block, 2 * depth)
            turned = jnp.concatenate([left[:, depth:], -left[:, :depth]], axis=1)
            left_h, left_l = split(jnp.concatenate([left, turned], axis=0))
            result = dot(left_h, right_h) + (dot(left_h, right_l) + dot(left_l, right_h))
            for c in range(2):
                part_ref[side, chunk, :, c * full : (c + 1) * full] = result[
                    c * block : (c + 1) * block
                ].reshape(group, 8, full)
            return carry

        lax.fori_loop(0, blocks, gram_block, 0)

    to_pair = pltpu.make_async_remote_copy(
        src_ref=part_ref.at[other], dst_ref=pair_ref, send_sem=pair_send, recv_sem=pair_recv,
        device_id=(2 * chip + other,), device_id_type=MESH,
    )
    gram(other)
    to_pair.start()
    gram(core)
    to_pair.wait_recv()

    def add_pair(k, carry):
        j = jnp.bitwise_xor(chip, chips - k)
        part_ref[core, j] = part_ref[core, j] + pair_ref[j]
        pltpu.make_async_remote_copy(
            src_ref=part_ref.at[core, j], dst_ref=rows_ref.at[chip], send_sem=row_send,
            recv_sem=row_recv, device_id=(2 * j + core,), device_id_type=MESH,
        ).start()
        return carry

    lax.fori_loop(1, chips, add_pair, 0)
    part_ref[core, chip] = part_ref[core, chip] + pair_ref[chip]
    pltpu.make_async_copy(part_ref.at[core, chip], rows_ref.at[chip], row_recv).start()
    rest = pl.ds(0, chips - 1)
    pltpu.make_async_copy(rows_ref, rows_ref, row_recv).wait()
    others = send.at[pl.ds(0, n - 1)]
    pltpu.make_async_copy(others, others, send_sem).wait()
    to_pair.wait_send()
    pltpu.make_async_copy(rows_ref.at[rest], rows_ref.at[rest], row_send).wait()


def local(n, state_real, state_imag, subsystem):
    amps = state_real.shape[0]
    vregs = amps // 1024
    width = vregs // n
    full = 8 * n
    chunk = (n, 8, 2 * width * 128)
    out = pl.pallas_call(
        functools.partial(exchange_kernel, n),
        out_shape=jax.ShapeDtypeStruct((n // 2, 8, 2 * full), jnp.float32),
        in_specs=[
            pl.BlockSpec(memory_space=pl.ANY),
            pl.BlockSpec(memory_space=pl.ANY),
            pl.BlockSpec(memory_space=pl.ANY),
        ],
        out_specs=pl.BlockSpec(memory_space=pl.ANY),
        scratch_shapes=[
            pltpu.SMEM((3,), jnp.int32),
            pltpu.VMEM((2, vregs, 8, 128), jnp.float32),
            pltpu.VMEM((2, vregs, 8, 128), jnp.float32),
            pltpu.VMEM(chunk, jnp.float32),
            pltpu.VMEM((n // 2, 2) + chunk[1:], jnp.float32),
            pltpu.VMEM((2, n // 2, 8, 2 * full), jnp.float32),
            pltpu.VMEM((n // 2, 8, 2 * full), jnp.float32),
            pltpu.SemaphoreType.DMA((3,)),
        ]
        + [pltpu.SemaphoreType.DMA] * 6,
        compiler_params=pltpu.CompilerParams(
            collective_id=0, has_side_effects=True, vmem_limit_bytes=56 * 2**20
        ),
    )(subsystem, state_real.reshape(vregs, 8, 128), state_imag.reshape(vregs, 8, 128))
    total = jnp.sum(out, axis=0) * (8.0 / amps)
    return total[:, :full], total[:, full:]


def solution(mesh):
    return jax.shard_map(
        functools.partial(local, mesh.shape["dev"]),
        mesh=mesh,
        in_specs=(P("dev"), P("dev"), P()),
        out_specs=(P("dev", None), P("dev", None)),
        check_vma=False,
    )
```

profile of v0, /device:TPU:0, one launch (start us, length us, event | category | flops | bytes accessed | tf_op | source)
XLA Modules:
  0.0 41.0 jit_solution(652814598960583497)
XLA Ops:
  0.6 38.8 %shard_map.50 = f32[16,8,512]{2,1,0:T(8,128)} custom-call(s32[3]{0:T(128)} %sub_hbm.1, f32[128,8,128]{2,1,0:T(8,128)} %bitcast.2, f32[128,8,128]{2,1,0:T(8,128)} %bitcast.3), custom_call_target="tpu_custom_call" | custom-call | tf_op jit(solution)/shard_map/pallas_call | solution.py:194
  39.4 1.0 %reduce_sum.9 = f32[8,512]{1,0:T(8,128)S(1)} reduce(f32[16,8,512]{2,1,0:T(8,128)} %shard_map.50, f32[]{:T(128)} %constant.0.clone.1), dimensions={0}, to_apply=%region_0.0 | reduce | flops 61440 | bytes 278532 | tf_op jit(solution)/shard_map/reduce_sum | solution.py:218
  40.4 0.6 %fusion = (f32[8,256]{1,0:T(8,128)}, f32[8,256]{1,0:T(8,128)}) fusion(f32[8,512]{1,0:T(8,128)S(1)} %broadcast_multiply_fusion), kind=kLoop, calls=%fused_computation.1 | loop fusion | bytes 32768 | tf_op jit(solution)/shard_map/slice | solution.py:219
  (1 shorter events, 0.0 us)
where the time goes:
time: 41.2 us; the launch traced here: 41 us
  Pallas kernels  38.8 us (94%)
  other arithmetic  0.98 us (2%)
  between operations  0.65 us (2%)
  local copies, waits for them, and re-layouts  0.61 us (1%)
    pallas_call x1, Pallas kernels, local(): pl.pallas_call(functools.partial(exchange_kernel, n), out_shape=jax.Shape...  38.8 us
    reduce_sum x1, other arithmetic, local(): total = jnp.sum(out, axis=0) * (8.0 / amps)  0.98 us

commit v1 on v0

v1 whole, which is shorter than its diff:
```python
import functools

import jax
import jax.numpy as jnp
from jax import lax
from jax.experimental import pallas as pl
from jax.experimental.pallas import tpu as pltpu
from jax.sharding import PartitionSpec as P

MESH = pl.DeviceIdType.MESH
PLANES = 4


def exchange_kernel(n, scale, sub_hbm, re_hbm, im_hbm, out_ref, sub_ref, state, mixed, send, recv,
                    high_ref, low_ref, part, turned_ref, chain, rows, load_sem, send_sem,
                    recv_sem, chain_sem, row_send, row_recv):
    me = lax.axis_index("dev")
    loads = [
        pltpu.make_async_copy(sub_hbm, sub_ref, load_sem.at[2]),
        pltpu.make_async_copy(re_hbm, state.at[0], load_sem.at[0]),
        pltpu.make_async_copy(im_hbm, state.at[1], load_sem.at[1]),
    ]
    for load in loads:
        load.start()
    barrier = pltpu.get_barrier_semaphore()

    def greet(k, carry):
        pl.semaphore_signal(
            barrier, inc=1, device_id=(jnp.bitwise_xor(me, n - k),), device_id_type=MESH
        )
        return carry

    lax.fori_loop(1, n, greet, 0)

    devs = n // PLANES
    chips = devs // 2
    owners = n // 2
    plane = me // devs
    chip = lax.rem(me, devs) // 2
    core = lax.rem(me, 2)
    low_half = plane < 2
    outer = (plane == 0) | (plane == PLANES - 1)
    inner = jnp.logical_not(outer)
    beside = jnp.bitwise_xor(plane, 1)
    far = jnp.where(low_half, 3, 0)
    across = jnp.where(low_half, 2, 1)

    vregs = state.shape[1]
    quarter = vregs // 4
    bits = vregs.bit_length() - 1
    width = vregs // owners
    full = 8 * n

    for load in loads:
        load.wait()

    lane = lax.broadcasted_iota(jnp.int32, (8, 128), 1)
    sub = lax.broadcasted_iota(jnp.int32, (8, 128), 0)

    mid = sub_ref[1]
    lane_step = jnp.int32(1)
    for b in range(1, 7):
        lane_step = jnp.where(mid == b, 2**b, lane_step)
    top = 10 + bits - 1
    in_lane = (mid < 7) | (mid == top - 1)
    stride = jnp.int32(vregs // 8)
    for b in range(10, top - 1):
        stride = jnp.where(mid == b, 2 ** (b - 10), stride)
    stride = jnp.where(mid == 7, vregs // 4, stride)
    stride = jnp.where(mid == 9, vregs // 2, stride)
    fixed = mid == 8
    lane_on = jnp.where(in_lane, lane_step, 0)
    lane_hit = jnp.bitwise_and(lane, lane_on) != 0
    lane_keep = lane_hit | (jnp.where(in_lane, 0, 1) != jnp.bitwise_and(lane, 0))
    sub_on = jnp.where(fixed, 0, 2)
    sub_hit = jnp.bitwise_and(sub, sub_on) != 0
    sub_keep = sub_hit | (jnp.where(fixed, 1, 0) != jnp.bitwise_and(sub, 0))

    high4 = sub >= 4
    odd_sub = jnp.bitwise_and(sub, 1) != 0
    odd_lane = jnp.bitwise_and(lane, 1) != 0

    def swap(a, b, hit, keep, step, axis):
        size = (8, 128)[axis]
        back = size - step
        return (
            jnp.where(hit, pltpu.roll(b, step, axis), a),
            jnp.where(keep, b, pltpu.roll(a, back, axis)),
        )

    def first_pass(v, carry):
        for c in range(2):
            x = [state[c, v + quarter * k] for k in range(4)]
            x[0], x[2] = swap(x[0], x[2], high4, high4, 4, 0)
            x[1], x[3] = swap(x[1], x[3], high4, high4, 4, 0)
            for k in (0, 2):
                a, b = swap(x[k], x[k + 1], odd_lane, odd_lane, 1, 1)
                x[k], x[k + 1] = swap(a, b, odd_sub, odd_sub, 1, 0)
            for k in range(4):
                mixed[c, v + quarter * k] = x[k]
        return carry

    lax.fori_loop(0, quarter, first_pass, 0, unroll=4)

    pairs = width // 2
    order = (
        jnp.where(outer, far, beside),
        jnp.where(outer, across, plane),
        jnp.where(outer, beside, far),
        jnp.where(outer, plane, across),
    )

    def target(k):
        at = k // chips
        zone = order[3]
        for i in (2, 1, 0):
            zone = jnp.where(at == i, order[i], zone)
        return zone, jnp.bitwise_xor(chip, chips - 1 - lax.rem(k, chips))

    def pack(k, carry):
        zone, where = target(k)
        owner = zone * chips + where
        for c in range(2):
            for p in range(pairs):
                u = owner * pairs + p
                low = jnp.bitwise_and(u, stride - 1)
                first = 2 * u - low
                a = mixed[c, first]
                b = mixed[c, first + stride]
                a, b = swap(a, b, lane_hit, lane_keep, lane_step, 1)
                a, b = swap(a, b, sub_hit, sub_keep, 2, 0)
                for w, value in enumerate((a, b)):
                    column = (c * width + 2 * p + w) * 128
                    send[owner, :, column : column + 128] = value
        return carry

    lax.fori_loop(0, chips, pack, 0)
    pl.semaphore_wait(barrier, n - 1)

    def send_chunk(k, carry):
        zone, where = target(k)
        owner = zone * chips + where
        device = zone * devs + 2 * where + 1

        @pl.when(device != me)
        def _():
            pltpu.make_async_remote_copy(
                src_ref=send.at[owner], dst_ref=recv.at[me], send_sem=send_sem,
                recv_sem=recv_sem.at[plane], device_id=(device,), device_id_type=MESH,
            ).start()

        @pl.when(device == me)
        def _():
            pltpu.make_async_copy(send.at[owner], recv.at[me], recv_sem.at[plane]).start()

        return carry

    def send_and_pack(k, carry):
        send_chunk(k, 0)
        pack(k + chips, 0)
        return carry

    lax.fori_loop(0, owners - chips, send_and_pack, 0)
    lax.fori_loop(owners - chips, owners, send_chunk, 0)

    depth = width * 128
    block = 8 * devs
    wide = max(block, 128)
    ratio = wide // block

    def split(x):
        high = x.astype(jnp.bfloat16)
        return high, (x - high.astype(jnp.float32)).astype(jnp.bfloat16)

    def dot(x, y):
        return lax.dot_general(x, y, (((1,), (1,)), ((), ())), preferred_element_type=jnp.float32)

    def stacked(x):
        return jnp.concatenate(
            [x, jnp.concatenate([x[:, depth:], -x[:, :depth]], axis=1)], axis=0
        )

    def arrival(s):
        second = jnp.where(outer, beside, far)
        third = jnp.where(outer, far, beside)
        return jnp.where(
            s == 0, plane, jnp.where(s == 1, second, jnp.where(s == 2, third, across))
        )

    def gram(s, carry):
        zone = arrival(s)
        mine = pl.ds(zone * devs, devs)
        lines = pl.ds(pl.multiple_of(zone * block, block), block)
        came = recv.at[mine]
        pltpu.make_async_copy(came, came, recv_sem.at[zone]).wait()
        high, low = split(recv[mine].reshape(block, 2 * depth))
        high_ref[lines] = high
        low_ref[lines] = low
        left_h = stacked(high)
        left_l = stacked(low)
        right_h = high_ref[...]
        result = dot(left_h, right_h) + (dot(left_h, low_ref[...]) + dot(left_l, right_h))
        column = pl.ds(pl.multiple_of(zone // ratio * wide, wide), wide)
        for c in range(2):
            value = result[c * block : (c + 1) * block]
            part[mine, :, c * full : (c + 1) * full] = value.reshape(devs, 8, full)
            if c == 1:
                value = -value
            if ratio > 1:
                slot = lax.rem(zone, ratio)
                value = jnp.concatenate(
                    [jnp.where(slot == r, value, 0.0) for r in range(ratio)], axis=0
                )
            turned_ref[c] = value.T.reshape(n, 8, wide)

        def mirror(e, carry):
            there = pl.ds(arrival(e) * devs, devs)
            for c in range(2):
                at = pl.ds(pl.multiple_of(c * full + zone // ratio * wide, wide), wide)
                part[there, :, at] = part[there, :, at] + turned_ref[c, there]
            return carry

        lax.fori_loop(0, s, mirror, 0)
        return carry

    def send_rows(zone, slot, ready):
        def one(k, carry):
            at = jnp.bitwise_xor(lax.rem(me, devs), devs - 1 - k)
            device = zone * devs + at
            ready(device)

            @pl.when(device != me)
            def _():
                pltpu.make_async_remote_copy(
                    src_ref=part.at[device], dst_ref=rows.at[slot, chip], send_sem=row_send,
                    recv_sem=row_recv.at[slot], device_id=(device,), device_id_type=MESH,
                ).start()

            @pl.when(device == me)
            def _():
                pltpu.make_async_copy(
                    part.at[device], rows.at[slot, chip], row_recv.at[slot]
                ).start()

            return carry

        lax.fori_loop(0, devs, one, 0)

    def add_chain(device):
        part[device] = part[device] + chain[device]

    @pl.when(core == 1)
    def _():
        high_ref[...] = jnp.zeros_like(high_ref)
        low_ref[...] = jnp.zeros_like(low_ref)
        lax.fori_loop(0, PLANES, gram, 0)

        @pl.when(outer)
        def _():
            for i, zone in enumerate((far, across, beside)):
                mine = pl.ds(zone * devs, devs)
                pltpu.make_async_remote_copy(
                    src_ref=part.at[mine], dst_ref=chain.at[mine], send_sem=row_send,
                    recv_sem=chain_sem.at[i], device_id=(beside * devs + 2 * chip + 1,),
                    device_id_type=MESH,
                ).start()
            send_rows(plane, 0, lambda device: None)

        @pl.when(inner)
        def _():
            send_rows(beside, 1, lambda device: None)
            for i, (zone, slot) in enumerate(((far, 2), (across, 2), (plane, 0))):
                came = chain.at[pl.ds(zone * devs, devs)]
                pltpu.make_async_copy(came, came, chain_sem.at[i]).wait()
                send_rows(zone, slot, add_chain)

    def gathered(slot):
        pltpu.make_async_copy(rows.at[slot], rows.at[slot], row_recv.at[slot]).wait()
        total = rows[slot, 0]
        for k in range(1, chips):
            total = total + rows[slot, k]
        return total

    out_ref[...] = gathered(0)

    @pl.when(outer)
    def _():
        out_ref[...] = out_ref[...] + gathered(1)

    out_ref[...] = (out_ref[...] + gathered(2)) * scale

    rest = send.at[pl.ds(0, owners - 1)]
    pltpu.make_async_copy(rest, rest, send_sem).wait()

    @pl.when(core == 0)
    def _():
        pltpu.make_async_copy(send.at[0], send.at[0], send_sem).wait()

    @pl.when(core == 1)
    def _():
        sent = part.at[pl.ds(0, n - 1)]
        pltpu.make_async_copy(sent, sent, row_send).wait()


def local(n, state_real, state_imag, subsystem):
    amps = state_real.shape[0]
    vregs = amps // 1024
    owners = n // 2
    width = vregs // owners
    full = 8 * n
    devs = n // PLANES
    wide = max(8 * devs, 128)
    chunk = (8, 2 * width * 128)
    out = pl.pallas_call(
        functools.partial(exchange_kernel, n, 8.0 / amps),
        out_shape=jax.ShapeDtypeStruct((8, 2 * full), jnp.float32),
        in_specs=[
            pl.BlockSpec(memory_space=pl.ANY),
            pl.BlockSpec(memory_space=pl.ANY),
            pl.BlockSpec(memory_space=pl.ANY),
        ],
        out_specs=pl.BlockSpec(memory_space=pltpu.VMEM),
        scratch_shapes=[
            pltpu.SMEM((3,), jnp.int32),
            pltpu.VMEM((2, vregs, 8, 128), jnp.float32),
            pltpu.VMEM((2, vregs, 8, 128), jnp.float32),
            pltpu.VMEM((owners,) + chunk, jnp.float32),
            pltpu.VMEM((n,) + chunk, jnp.float32),
            pltpu.VMEM((full, chunk[1]), jnp.bfloat16),
            pltpu.VMEM((full, chunk[1]), jnp.bfloat16),
            pltpu.VMEM((n, 8, 2 * full), jnp.float32),
            pltpu.VMEM((2, n, 8, wide), jnp.float32),
            pltpu.VMEM((n, 8, 2 * full), jnp.float32),
            pltpu.VMEM((3, devs // 2, 8, 2 * full), jnp.float32),
            pltpu.SemaphoreType.DMA((3,)),
            pltpu.SemaphoreType.DMA,
            pltpu.SemaphoreType.DMA((PLANES,)),
            pltpu.SemaphoreType.DMA((3,)),
            pltpu.SemaphoreType.DMA,
            pltpu.SemaphoreType.DMA((3,)),
        ],
        compiler_params=pltpu.CompilerParams(
            collective_id=0, has_side_effects=True, vmem_limit_bytes=56 * 2**20
        ),
    )(subsystem, state_real.reshape(vregs, 8, 128), state_imag.reshape(vregs, 8, 128))
    return out[:, :full], out[:, full:]


def solution(mesh):
    return jax.shard_map(
        functools.partial(local, mesh.shape["dev"]),
        mesh=mesh,
        in_specs=(P("dev"), P("dev"), P()),
        out_specs=(P("dev", None), P("dev", None)),
        check_vma=False,
    )
```

time: 41.2 us -> 40 us (0.971)
  other arithmetic: 0.98 us -> 0 us
  Pallas kernels: 38.8 us -> 37.9 us
  local copies, waits for them, and re-layouts: 0.61 us -> 1.32 us
    reduce_sum x1 -> x0, other arithmetic: 0.98 us -> none  [local(): total = jnp.sum(out, axis=0) * (8.0 / amps)]
    pallas_call x1, Pallas kernels: 38.8 us -> 37.9 us  [local(): pl.pallas_call(functools.partial(exchange_kernel, n, 8.0 / amps), out_sha...]
    slice x1, local copies, waits for them, and re-layouts: 0.61 us -> 1.32 us  [local(): return (out[:, :full], out[:, full:])]
where the time goes in v1:
time: 40 us; the launch traced here: 39.8 us
  Pallas kernels  37.9 us (95%)
  local copies, waits for them, and re-layouts  1.32 us (3%)
  between operations  0.64 us (2%)
    pallas_call x1, Pallas kernels, local(): pl.pallas_call(functools.partial(exchange_kernel, n, 8.0 / amps), out_sha...  37.9 us
    slice x1, local copies, waits for them, and re-layouts, local(): return (out[:, :full], out[:, full:])  1.32 us

profile of v1, /device:TPU:0, one launch (start us, length us, event | category | flops | bytes accessed | tf_op | source)
XLA Modules:
  0.0 39.8 jit_solution(11704004452455716988)
XLA Ops:
  0.6 37.9 %shard_map.50 = f32[8,512]{1,0:T(8,128)} custom-call(s32[3]{0:T(128)} %sub_hbm.1, f32[128,8,128]{2,1,0:T(8,128)} %bitcast.2, f32[128,8,128]{2,1,0:T(8,128)} %bitcast.3), custom_call_target="tpu_custom_call" | custom-call | tf_op jit(solution)/shard_map/pallas_call | solution.py:314
  38.5 1.3 %fusion = (f32[8,256]{1,0:T(8,128)}, f32[8,256]{1,0:T(8,128)}) fusion(f32[8,512]{1,0:T(8,128)} %shard_map.50), kind=kLoop, calls=%fused_computation | loop fusion | bytes 32768 | tf_op jit(solution)/shard_map/slice | solution.py:346

commit v2 on v1

--- a/solution.py
+++ b/solution.py
@@ -100,7 +100,7 @@
                 mixed[c, v + quarter * k] = x[k]
         return carry
 
-    lax.fori_loop(0, quarter, first_pass, 0, unroll=4)
+    lax.fori_loop(0, quarter, first_pass, 0, unroll=32)
 
     pairs = width // 2
     order = (
@@ -134,7 +134,8 @@
                     send[owner, :, column : column + 128] = value
         return carry
 
-    lax.fori_loop(0, chips, pack, 0)
+    together = min(chips, 4)
+    lax.fori_loop(0, chips, pack, 0, unroll=together)
     pl.semaphore_wait(barrier, n - 1)
 
     def send_chunk(k, carry):
@@ -155,12 +156,16 @@
 
         return carry
 
-    def send_and_pack(k, carry):
-        send_chunk(k, 0)
-        pack(k + chips, 0)
-        return carry
-
-    lax.fori_loop(0, owners - chips, send_and_pack, 0)
+    def send_and_pack(i, carry):
+        lax.fori_loop(i * chips, (i + 1) * chips, send_chunk, 0)
+
+        def pack_next(k, carry):
+            return pack((i + 1) * chips + k, carry)
+
+        lax.fori_loop(0, chips, pack_next, 0, unroll=together)
+        return carry
+
+    lax.fori_loop(0, PLANES - 1, send_and_pack, 0)
     lax.fori_loop(owners - chips, owners, send_chunk, 0)
 
     depth = width * 128
@@ -313,7 +318,7 @@
     chunk = (8, 2 * width * 128)
     out = pl.pallas_call(
         functools.partial(exchange_kernel, n, 8.0 / amps),
-        out_shape=jax.ShapeDtypeStruct((8, 2 * full), jnp.float32),
+        out_shape=pltpu.VMEM((8, 2 * full), jnp.float32),
         in_specs=[
             pl.BlockSpec(memory_space=pl.ANY),
             pl.BlockSpec(memory_space=pl.ANY),

time: 40 us -> 38.2 us (0.955)
  Pallas kernels: 37.9 us -> 36.8 us
  local copies, waits for them, and re-layouts: 1.32 us -> 0.61 us
    pallas_call x1, Pallas kernels: 37.9 us -> 36.8 us  [local(): pl.pallas_call(functools.partial(exchange_kernel, n, 8.0 / amps), out_sha...]
    slice x1, local copies, waits for them, and re-layouts: 1.32 us -> 0.61 us  [local(): return (out[:, :full], out[:, full:])]
where the time goes in v2:
time: 38.2 us; the launch traced here: 38 us
  Pallas kernels  36.8 us (96%)
  between operations  0.64 us (2%)
  local copies, waits for them, and re-layouts  0.61 us (2%)
    pallas_call x1, Pallas kernels, local(): pl.pallas_call(functools.partial(exchange_kernel, n, 8.0 / amps), out_sha...  36.8 us

profile of v2, /device:TPU:0, one launch (start us, length us, event | category | flops | bytes accessed | tf_op | source)
XLA Modules:
  0.0 38.0 jit_solution(5771738282495217291)
XLA Ops:
  0.6 36.8 %shard_map.50 = f32[8,512]{1,0:T(8,128)S(1)} custom-call(s32[3]{0:T(128)} %sub_hbm.1, f32[128,8,128]{2,1,0:T(8,128)} %bitcast.2, f32[128,8,128]{2,1,0:T(8,128)} %bitcast.3), custom_call_target="tpu_custom_call" | custom-call | tf_op jit(solution)/shard_map/pallas_call | solution.py:319
  37.4 0.6 %fusion = (f32[8,256]{1,0:T(8,128)}, f32[8,256]{1,0:T(8,128)}) fusion(f32[8,512]{1,0:T(8,128)S(1)} %shard_map.50), kind=kLoop, calls=%fused_computation | loop fusion | bytes 32768 | tf_op jit(solution)/shard_map/slice | solution.py:351

commit v3 on v2

--- a/solution.py
+++ b/solution.py
@@ -13,7 +13,7 @@
 
 def exchange_kernel(n, scale, sub_hbm, re_hbm, im_hbm, out_ref, sub_ref, state, mixed, send, recv,
                     high_ref, low_ref, part, turned_ref, chain, rows, load_sem, send_sem,
-                    recv_sem, chain_sem, row_send, row_recv):
+                    recv_sem, chain_sem, row_send, row_recv, present):
     me = lax.axis_index("dev")
     loads = [
         pltpu.make_async_copy(sub_hbm, sub_ref, load_sem.at[2]),
@@ -24,13 +24,15 @@
         load.start()
     barrier = pltpu.get_barrier_semaphore()
 
-    def greet(k, carry):
-        pl.semaphore_signal(
-            barrier, inc=1, device_id=(jnp.bitwise_xor(me, n - k),), device_id_type=MESH
-        )
-        return carry
-
-    lax.fori_loop(1, n, greet, 0)
+    @pl.when(lax.rem(me, 2) == 1)
+    def _():
+        def greet(k, carry):
+            pl.semaphore_signal(
+                barrier, inc=1, device_id=(jnp.bitwise_xor(me, n - k),), device_id_type=MESH
+            )
+            return carry
+
+        lax.fori_loop(1, n, greet, 0)
 
     devs = n // PLANES
     chips = devs // 2
@@ -104,9 +106,9 @@
 
     pairs = width // 2
     order = (
-        jnp.where(outer, far, beside),
-        jnp.where(outer, across, plane),
-        jnp.where(outer, beside, far),
+        far,
+        jnp.where(outer, across, beside),
+        jnp.where(outer, beside, plane),
         jnp.where(outer, plane, across),
     )
 
@@ -136,7 +138,7 @@
 
     together = min(chips, 4)
     lax.fori_loop(0, chips, pack, 0, unroll=together)
-    pl.semaphore_wait(barrier, n - 1)
+    pl.semaphore_wait(barrier, owners - core)
 
     def send_chunk(k, carry):
         zone, where = target(k)
@@ -167,6 +169,17 @@
 
     lax.fori_loop(0, PLANES - 1, send_and_pack, 0)
     lax.fori_loop(owners - chips, owners, send_chunk, 0)
+
+    @pl.when(core == 0)
+    def _():
+        def tell(k, carry):
+            pl.semaphore_signal(
+                present, inc=1, device_id=(2 * k + 1,), device_id_type=MESH
+            )
+            return carry
+
+        lax.fori_loop(0, owners, tell, 0)
+
 
     depth = width * 128
     block = 8 * devs
@@ -202,9 +215,8 @@
         high_ref[lines] = high
         low_ref[lines] = low
         left_h = stacked(high)
-        left_l = stacked(low)
-        right_h = high_ref[...]
-        result = dot(left_h, right_h) + (dot(left_h, low_ref[...]) + dot(left_l, right_h))
+        both = dot(jnp.concatenate([left_h, stacked(low)], axis=0), high_ref[...])
+        result = both[: 2 * block] + (both[2 * block :] + dot(left_h, low_ref[...]))
         column = pl.ds(pl.multiple_of(zone // ratio * wide, wide), wide)
         for c in range(2):
             value = result[c * block : (c + 1) * block]
@@ -230,8 +242,7 @@
 
     def send_rows(zone, slot, ready):
         def one(k, carry):
-            at = jnp.bitwise_xor(lax.rem(me, devs), devs - 1 - k)
-            device = zone * devs + at
+            device = zone * devs + k
             ready(device)
 
             @pl.when(device != me)
@@ -256,6 +267,7 @@
 
     @pl.when(core == 1)
     def _():
+        pl.semaphore_wait(present, owners)
         high_ref[...] = jnp.zeros_like(high_ref)
         low_ref[...] = jnp.zeros_like(low_ref)
         lax.fori_loop(0, PLANES, gram, 0)
@@ -273,11 +285,12 @@
 
         @pl.when(inner)
         def _():
-            send_rows(beside, 1, lambda device: None)
             for i, (zone, slot) in enumerate(((far, 2), (across, 2), (plane, 0))):
                 came = chain.at[pl.ds(zone * devs, devs)]
                 pltpu.make_async_copy(came, came, chain_sem.at[i]).wait()
                 send_rows(zone, slot, add_chain)
+                if i == 0:
+                    send_rows(beside, 1, lambda device: None)
 
     def gathered(slot):
         pltpu.make_async_copy(rows.at[slot], rows.at[slot], row_recv.at[slot]).wait()
@@ -343,6 +356,7 @@
             pltpu.SemaphoreType.DMA((3,)),
             pltpu.SemaphoreType.DMA,
             pltpu.SemaphoreType.DMA((3,)),
+            pltpu.SemaphoreType.REGULAR,
         ],
         compiler_params=pltpu.CompilerParams(
             collective_id=0, has_side_effects=True, vmem_limit_bytes=56 * 2**20

time: 38.2 us -> 36 us (0.942)
  Pallas kernels: 36.8 us -> 34.4 us
    pallas_call x1, Pallas kernels: 36.8 us -> 34.4 us  [local(): pl.pallas_call(functools.partial(exchange_kernel, n, 8.0 / amps), out_sha...]
where the time goes in v3:
time: 36 us; the launch traced here: 35.7 us
  Pallas kernels  34.4 us (96%)
  between operations  0.64 us (2%)
  local copies, waits for them, and re-layouts  0.61 us (2%)
    pallas_call x1, Pallas kernels, local(): pl.pallas_call(functools.partial(exchange_kernel, n, 8.0 / amps), out_sha...  34.4 us

profile of v3, /device:TPU:0, one launch (start us, length us, event | category | flops | bytes accessed | tf_op | source)
XLA Modules:
  0.0 35.7 jit_solution(9237243118744255658)
XLA Ops:
  0.6 34.4 %shard_map.50 = f32[8,512]{1,0:T(8,128)S(1)} custom-call(s32[3]{0:T(128)} %sub_hbm.1, f32[128,8,128]{2,1,0:T(8,128)} %bitcast.2, f32[128,8,128]{2,1,0:T(8,128)} %bitcast.3), custom_call_target="tpu_custom_call" | custom-call | tf_op jit(solution)/shard_map/pallas_call | solution.py:332
  35.1 0.6 %fusion = (f32[8,256]{1,0:T(8,128)}, f32[8,256]{1,0:T(8,128)}) fusion(f32[8,512]{1,0:T(8,128)S(1)} %shard_map.50), kind=kLoop, calls=%fused_computation | loop fusion | bytes 32768 | tf_op jit(solution)/shard_map/slice | solution.py:365

commit v4 on v3

--- a/solution.py
+++ b/solution.py
@@ -53,8 +53,7 @@
     width = vregs // owners
     full = 8 * n
 
-    for load in loads:
-        load.wait()
+    loads[0].wait()
 
     lane = lax.broadcasted_iota(jnp.int32, (8, 128), 1)
     sub = lax.broadcasted_iota(jnp.int32, (8, 128), 0)
@@ -90,8 +89,10 @@
             jnp.where(keep, b, pltpu.roll(a, back, axis)),
         )
 
-    def first_pass(v, carry):
-        for c in range(2):
+    for c in range(2):
+        loads[1 + c].wait()
+
+        def first_pass(v, carry):
             x = [state[c, v + quarter * k] for k in range(4)]
             x[0], x[2] = swap(x[0], x[2], high4, high4, 4, 0)
             x[1], x[3] = swap(x[1], x[3], high4, high4, 4, 0)
@@ -100,11 +101,13 @@
                 x[k], x[k + 1] = swap(a, b, odd_sub, odd_sub, 1, 0)
             for k in range(4):
                 mixed[c, v + quarter * k] = x[k]
-        return carry
-
-    lax.fori_loop(0, quarter, first_pass, 0, unroll=32)
+            return carry
+
+        lax.fori_loop(0, quarter, first_pass, 0, unroll=32)
 
     pairs = width // 2
+    tiles = width // 2
+    depth = tiles * 128
     order = (
         far,
         jnp.where(outer, across, beside),
@@ -132,34 +135,41 @@
                 a, b = swap(a, b, lane_hit, lane_keep, lane_step, 1)
                 a, b = swap(a, b, sub_hit, sub_keep, 2, 0)
                 for w, value in enumerate((a, b)):
-                    column = (c * width + 2 * p + w) * 128
-                    send[owner, :, column : column + 128] = value
+                    half, tile = divmod(2 * p + w, tiles)
+                    column = (c * tiles + tile) * 128
+                    send[owner, half, :, column : column + 128] = value
         return carry
 
     together = min(chips, 4)
     lax.fori_loop(0, chips, pack, 0, unroll=together)
     pl.semaphore_wait(barrier, owners - core)
 
-    def send_chunk(k, carry):
-        zone, where = target(k)
-        owner = zone * chips + where
-        device = zone * devs + 2 * where + 1
-
-        @pl.when(device != me)
-        def _():
-            pltpu.make_async_remote_copy(
-                src_ref=send.at[owner], dst_ref=recv.at[me], send_sem=send_sem,
-                recv_sem=recv_sem.at[plane], device_id=(device,), device_id_type=MESH,
-            ).start()
-
-        @pl.when(device == me)
-        def _():
-            pltpu.make_async_copy(send.at[owner], recv.at[me], recv_sem.at[plane]).start()
-
-        return carry
+    def send_group(i):
+        def send_chunk(k, carry):
+            zone, where = target(i * chips + lax.rem(k, chips))
+            half = k // chips
+            owner = zone * chips + where
+            device = zone * devs + 2 * where + 1
+
+            @pl.when(device != me)
+            def _():
+                pltpu.make_async_remote_copy(
+                    src_ref=send.at[owner, half], dst_ref=recv.at[half, me], send_sem=send_sem,
+                    recv_sem=recv_sem.at[plane, half], device_id=(device,), device_id_type=MESH,
+                ).start()
+
+            @pl.when(device == me)
+            def _():
+                pltpu.make_async_copy(
+                    send.at[owner, half], recv.at[half, me], recv_sem.at[plane, half]
+                ).start()
+
+            return carry
+
+        lax.fori_loop(0, 2 * chips, send_chunk, 0)
 
     def send_and_pack(i, carry):
-        lax.fori_loop(i * chips, (i + 1) * chips, send_chunk, 0)
+        send_group(i)
 
         def pack_next(k, carry):
             return pack((i + 1) * chips + k, carry)
@@ -168,7 +178,7 @@
         return carry
 
     lax.fori_loop(0, PLANES - 1, send_and_pack, 0)
-    lax.fori_loop(owners - chips, owners, send_chunk, 0)
+    send_group(PLANES - 1)
 
     @pl.when(core == 0)
     def _():
@@ -181,10 +191,10 @@
         lax.fori_loop(0, owners, tell, 0)
 
 
-    depth = width * 128
     block = 8 * devs
     wide = max(block, 128)
     ratio = wide // block
+    columns = full // 2
 
     def split(x):
         high = x.astype(jnp.bfloat16)
@@ -199,28 +209,35 @@
         )
 
     def arrival(s):
-        second = jnp.where(outer, beside, far)
-        third = jnp.where(outer, far, beside)
+        second = jnp.where(outer, far, beside)
+        third = jnp.where(outer, across, far)
+        last = jnp.where(outer, beside, across)
         return jnp.where(
-            s == 0, plane, jnp.where(s == 1, second, jnp.where(s == 2, third, across))
+            s == 0, plane, jnp.where(s == 1, second, jnp.where(s == 2, third, last))
         )
 
-    def gram(s, carry):
-        zone = arrival(s)
+    def gram(step, carry):
+        zone = arrival(step // 2)
+        half = lax.rem(step, 2)
         mine = pl.ds(zone * devs, devs)
         lines = pl.ds(pl.multiple_of(zone * block, block), block)
-        came = recv.at[mine]
-        pltpu.make_async_copy(came, came, recv_sem.at[zone]).wait()
-        high, low = split(recv[mine].reshape(block, 2 * depth))
-        high_ref[lines] = high
-        low_ref[lines] = low
+        came = recv.at[half, mine]
+        pltpu.make_async_copy(came, came, recv_sem.at[zone, half]).wait()
+        high, low = split(recv[half, mine].reshape(block, 2 * depth))
+        high_ref[half, lines] = high
+        low_ref[half, lines] = low
         left_h = stacked(high)
-        both = dot(jnp.concatenate([left_h, stacked(low)], axis=0), high_ref[...])
-        result = both[: 2 * block] + (both[2 * block :] + dot(left_h, low_ref[...]))
-        column = pl.ds(pl.multiple_of(zone // ratio * wide, wide), wide)
+        both = dot(jnp.concatenate([left_h, stacked(low)], axis=0), high_ref[half])
+        result = both[: 2 * block] + (both[2 * block :] + dot(left_h, low_ref[half]))
+        start = lax.rem(zone * block, columns) // wide * wide
         for c in range(2):
             value = result[c * block : (c + 1) * block]
-            part[mine, :, c * full : (c + 1) * full] = value.reshape(devs, 8, full)
+            here = slice(c * columns, (c + 1) * columns)
+            for side in range(2):
+                piece = value[:, side * columns : (side + 1) * columns]
+                part[mine, side, :, here] = part[mine, side, :, here] + piece.reshape(
+                    devs, 8, columns
+                )
             if c == 1:
                 value = -value
             if ratio > 1:
@@ -233,30 +250,35 @@
         def mirror(e, carry):
             there = pl.ds(arrival(e) * devs, devs)
             for c in range(2):
-                at = pl.ds(pl.multiple_of(c * full + zone // ratio * wide, wide), wide)
-                part[there, :, at] = part[there, :, at] + turned_ref[c, there]
-            return carry
-
-        lax.fori_loop(0, s, mirror, 0)
+                at = pl.ds(pl.multiple_of(c * columns + start, 128), wide)
+                part[there, zone // 2, :, at] = (
+                    part[there, zone // 2, :, at] + turned_ref[c, there]
+                )
+            return carry
+
+        lax.fori_loop(0, step // 2, mirror, 0)
         return carry
 
-    def send_rows(zone, slot, ready):
+    def send_rows(zone, slot, half=None, ready=None):
         def one(k, carry):
             device = zone * devs + k
-            ready(device)
+            if ready is not None:
+                ready(device)
+            if half is None:
+                source, target_rows = part.at[device], rows.at[slot, chip]
+            else:
+                source, target_rows = part.at[device, half], rows.at[slot, chip, half]
 
             @pl.when(device != me)
             def _():
                 pltpu.make_async_remote_copy(
-                    src_ref=part.at[device], dst_ref=rows.at[slot, chip], send_sem=row_send,
+                    src_ref=source, dst_ref=target_rows, send_sem=row_send,
                     recv_sem=row_recv.at[slot], device_id=(device,), device_id_type=MESH,
                 ).start()
 
             @pl.when(device == me)
             def _():
-                pltpu.make_async_copy(
-                    part.at[device], rows.at[slot, chip], row_recv.at[slot]
-                ).start()
+                pltpu.make_async_copy(source, target_rows, row_recv.at[slot]).start()
 
             return carry
 
@@ -270,27 +292,38 @@
         pl.semaphore_wait(present, owners)
         high_ref[...] = jnp.zeros_like(high_ref)
         low_ref[...] = jnp.zeros_like(low_ref)
-        lax.fori_loop(0, PLANES, gram, 0)
+        part[...] = jnp.zeros_like(part)
+        lax.fori_loop(0, 2 * PLANES - 2, gram, 0)
+        near = plane // 2
+
+        @pl.when(inner)
+        def _():
+            send_rows(beside, 1, near)
+            send_rows(plane, 0, near)
+
+        lax.fori_loop(2 * PLANES - 2, 2 * PLANES, gram, 0)
 
         @pl.when(outer)
         def _():
-            for i, zone in enumerate((far, across, beside)):
+            for i, zone in enumerate((far, across)):
                 mine = pl.ds(zone * devs, devs)
                 pltpu.make_async_remote_copy(
                     src_ref=part.at[mine], dst_ref=chain.at[mine], send_sem=row_send,
                     recv_sem=chain_sem.at[i], device_id=(beside * devs + 2 * chip + 1,),
                     device_id_type=MESH,
                 ).start()
-            send_rows(plane, 0, lambda device: None)
+            send_rows(beside, 1)
+            send_rows(plane, 0)
 
         @pl.when(inner)
         def _():
-            for i, (zone, slot) in enumerate(((far, 2), (across, 2), (plane, 0))):
+            for i, zone in enumerate((far, across)):
                 came = chain.at[pl.ds(zone * devs, devs)]
                 pltpu.make_async_copy(came, came, chain_sem.at[i]).wait()
-                send_rows(zone, slot, add_chain)
+                send_rows(zone, 2, ready=add_chain)
                 if i == 0:
-                    send_rows(beside, 1, lambda device: None)
+                    send_rows(beside, 1, 1 - near)
+            send_rows(plane, 0, 1 - near)
 
     def gathered(slot):
         pltpu.make_async_copy(rows.at[slot], rows.at[slot], row_recv.at[slot]).wait()
@@ -299,13 +332,11 @@
             total = total + rows[slot, k]
         return total
 
-    out_ref[...] = gathered(0)
-
-    @pl.when(outer)
-    def _():
-        out_ref[...] = out_ref[...] + gathered(1)
-
-    out_ref[...] = (out_ref[...] + gathered(2)) * scale
+    total = (gathered(0) + gathered(1) + gathered(2)) * scale
+    for side in range(2):
+        for c in range(2):
+            at = c * full + side * columns
+            out_ref[:, at : at + columns] = total[side, :, c * columns : (c + 1) * columns]
 
     rest = send.at[pl.ds(0, owners - 1)]
     pltpu.make_async_copy(rest, rest, send_sem).wait()
@@ -328,7 +359,7 @@
     full = 8 * n
     devs = n // PLANES
     wide = max(8 * devs, 128)
-    chunk = (8, 2 * width * 128)
+    chunk = (8, width * 128)
     out = pl.pallas_call(
         functools.partial(exchange_kernel, n, 8.0 / amps),
         out_shape=pltpu.VMEM((8, 2 * full), jnp.float32),
@@ -342,18 +373,18 @@
             pltpu.SMEM((3,), jnp.int32),
             pltpu.VMEM((2, vregs, 8, 128), jnp.float32),
             pltpu.VMEM((2, vregs, 8, 128), jnp.float32),
-            pltpu.VMEM((owners,) + chunk, jnp.float32),
-            pltpu.VMEM((n,) + chunk, jnp.float32),
-            pltpu.VMEM((full, chunk[1]), jnp.bfloat16),
-            pltpu.VMEM((full, chunk[1]), jnp.bfloat16),
-            pltpu.VMEM((n, 8, 2 * full), jnp.float32),
+            pltpu.VMEM((owners, 2) + chunk, jnp.float32),
+            pltpu.VMEM((2, n) + chunk, jnp.float32),
+            pltpu.VMEM((2, full, chunk[1]), jnp.bfloat16),
+            pltpu.VMEM((2, full, chunk[1]), jnp.bfloat16),
+            pltpu.VMEM((n, 2, 8, full), jnp.float32),
             pltpu.VMEM((2, n, 8, wide), jnp.float32),
-            pltpu.VMEM((n, 8, 2 * full), jnp.float32),
-            pltpu.VMEM((3, devs // 2, 8, 2 * full), jnp.float32),
+            pltpu.VMEM((n, 2, 8, full), jnp.float32),
+            pltpu.VMEM((3, devs // 2, 2, 8, full), jnp.float32),
             pltpu.SemaphoreType.DMA((3,)),
             pltpu.SemaphoreType.DMA,
-            pltpu.SemaphoreType.DMA((PLANES,)),
-            pltpu.SemaphoreType.DMA((3,)),
+            pltpu.SemaphoreType.DMA((PLANES, 2)),
+            pltpu.SemaphoreType.DMA((2,)),
             pltpu.SemaphoreType.DMA,
             pltpu.SemaphoreType.DMA((3,)),
             pltpu.SemaphoreType.REGULAR,

time: 36 us -> 35.7 us (level)
  no operation moved by 1% of the time
where the time goes in v4:
time: 35.7 us; the launch traced here: 35.5 us
  Pallas kernels  34.3 us (96%)
  between operations  0.64 us (2%)
  local copies, waits for them, and re-layouts  0.61 us (2%)
    pallas_call x1, Pallas kernels, local(): pl.pallas_call(functools.partial(exchange_kernel, n, 8.0 / amps), out_sha...  34.3 us

profile of v4, /device:TPU:0, one launch (start us, length us, event | category | flops | bytes accessed | tf_op | source)
XLA Modules:
  0.0 35.5 jit_solution(18064074897778233883)
XLA Ops:
  0.6 34.3 %shard_map.50 = f32[8,512]{1,0:T(8,128)S(1)} custom-call(s32[3]{0:T(128)} %sub_hbm.1, f32[128,8,128]{2,1,0:T(8,128)} %bitcast.2, f32[128,8,128]{2,1,0:T(8,128)} %bitcast.3), custom_call_target="tpu_custom_call" | custom-call | tf_op jit(solution)/shard_map/pallas_call | solution.py:363
  34.9 0.6 %fusion = (f32[8,256]{1,0:T(8,128)}, f32[8,256]{1,0:T(8,128)}) fusion(f32[8,512]{1,0:T(8,128)S(1)} %shard_map.50), kind=kLoop, calls=%fused_computation | loop fusion | bytes 32768 | tf_op jit(solution)/shard_map/slice | solution.py:396

commit v5 on v4

--- a/solution.py
+++ b/solution.py
@@ -13,7 +13,7 @@
 
 def exchange_kernel(n, scale, sub_hbm, re_hbm, im_hbm, out_ref, sub_ref, state, mixed, send, recv,
                     high_ref, low_ref, part, turned_ref, chain, rows, load_sem, send_sem,
-                    recv_sem, chain_sem, row_send, row_recv, present):
+                    recv_sem, chain_sem, row_send, row_recv, present, outer_in, go):
     me = lax.axis_index("dev")
     loads = [
         pltpu.make_async_copy(sub_hbm, sub_ref, load_sem.at[2]),
@@ -23,16 +23,6 @@
     for load in loads:
         load.start()
     barrier = pltpu.get_barrier_semaphore()
-
-    @pl.when(lax.rem(me, 2) == 1)
-    def _():
-        def greet(k, carry):
-            pl.semaphore_signal(
-                barrier, inc=1, device_id=(jnp.bitwise_xor(me, n - k),), device_id_type=MESH
-            )
-            return carry
-
-        lax.fori_loop(1, n, greet, 0)
 
     devs = n // PLANES
     chips = devs // 2
@@ -46,6 +36,23 @@
     beside = jnp.bitwise_xor(plane, 1)
     far = jnp.where(low_half, 3, 0)
     across = jnp.where(low_half, 2, 1)
+
+    mate = jnp.bitwise_xor(me, 1)
+
+    def signal(sem, device):
+        pl.semaphore_signal(sem, inc=1, device_id=(device,), device_id_type=MESH)
+
+    @pl.when(inner & (core == 1))
+    def _():
+        def greet(k, carry):
+            signal(barrier, jnp.bitwise_xor(me, n - k))
+            return carry
+
+        lax.fori_loop(1, n, greet, 0)
+
+    @pl.when(outer | (core == 0))
+    def _():
+        signal(barrier, mate)
 
     vregs = state.shape[1]
     quarter = vregs // 4
@@ -108,23 +115,10 @@
     pairs = width // 2
     tiles = width // 2
     depth = tiles * 128
-    order = (
-        far,
-        jnp.where(outer, across, beside),
-        jnp.where(outer, beside, plane),
-        jnp.where(outer, plane, across),
-    )
-
-    def target(k):
-        at = k // chips
-        zone = order[3]
-        for i in (2, 1, 0):
-            zone = jnp.where(at == i, order[i], zone)
-        return zone, jnp.bitwise_xor(chip, chips - 1 - lax.rem(k, chips))
-
-    def pack(k, carry):
-        zone, where = target(k)
-        owner = zone * chips + where
+    def target(zone, k):
+        return zone * chips + jnp.bitwise_xor(chip, chips - 1 - k)
+
+    def pack(owner):
         for c in range(2):
             for p in range(pairs):
                 u = owner * pairs + p
@@ -138,18 +132,21 @@
                     half, tile = divmod(2 * p + w, tiles)
                     column = (c * tiles + tile) * 128
                     send[owner, half, :, column : column + 128] = value
-        return carry
-
-    together = min(chips, 4)
-    lax.fori_loop(0, chips, pack, 0, unroll=together)
-    pl.semaphore_wait(barrier, owners - core)
-
-    def send_group(i):
-        def send_chunk(k, carry):
-            zone, where = target(i * chips + lax.rem(k, chips))
-            half = k // chips
-            owner = zone * chips + where
-            device = zone * devs + 2 * where + 1
+
+    def pack_group(zone, start):
+        def one(k, carry):
+            pack(target(zone, k))
+            return carry
+
+        lax.fori_loop(start, chips, one, 0, unroll=4 - start if chips >= 4 else 1)
+
+    def send_group(zone, start, stop):
+        count = stop - start
+
+        def one(k, carry):
+            owner = target(zone, start + lax.rem(k, count))
+            half = k // count
+            device = 2 * owner + 1
 
             @pl.when(device != me)
             def _():
@@ -166,26 +163,48 @@
 
             return carry
 
-        lax.fori_loop(0, 2 * chips, send_chunk, 0)
-
-    def send_and_pack(i, carry):
-        send_group(i)
-
-        def pack_next(k, carry):
-            return pack((i + 1) * chips + k, carry)
-
-        lax.fori_loop(0, chips, pack_next, 0, unroll=together)
-        return carry
-
-    lax.fori_loop(0, PLANES - 1, send_and_pack, 0)
-    send_group(PLANES - 1)
+        lax.fori_loop(0, 2 * count, one, 0)
+
+    pack(target(across, 0))
+    pl.semaphore_wait(barrier, owners // 2 + jnp.where(outer, 1, 0))
+
+    @pl.when(outer & (core == 1))
+    def _():
+        def tell(k, carry):
+            signal(outer_in, devs + 2 * k + 1)
+            return carry
+
+        lax.fori_loop(0, owners // 2, tell, 0)
+
+    send_group(across, 0, 1)
+    pack_group(far, 0)
+
+    @pl.when(inner & (core == 1))
+    def _():
+        pl.semaphore_wait(outer_in, owners // 2)
+        signal(go, mate)
+        signal(go, beside * devs + 2 * chip + 1)
+
+    @pl.when(outer | (core == 0))
+    def _():
+        pl.semaphore_wait(go, 1)
+
+    @pl.when(outer & (core == 1))
+    def _():
+        signal(go, mate)
+
+    send_group(far, 0, chips)
+    pack_group(beside, 0)
+    send_group(beside, 0, chips)
+    pack_group(across, 1)
+    send_group(across, 1, chips)
+    pack_group(plane, 0)
+    send_group(plane, 0, chips)
 
     @pl.when(core == 0)
     def _():
         def tell(k, carry):
-            pl.semaphore_signal(
-                present, inc=1, device_id=(2 * k + 1,), device_id_type=MESH
-            )
+            signal(present, 2 * k + 1)
             return carry
 
         lax.fori_loop(0, owners, tell, 0)
@@ -217,8 +236,10 @@
         )
 
     def gram(step, carry):
-        zone = arrival(step // 2)
-        half = lax.rem(step, 2)
+        crossed = outer & (step >= 4)
+        at = jnp.where(crossed, 2 + lax.rem(step, 2), step // 2)
+        half = jnp.where(crossed, step // 2 - 2, lax.rem(step, 2))
+        zone = arrival(at)
         mine = pl.ds(zone * devs, devs)
         lines = pl.ds(pl.multiple_of(zone * block, block), block)
         came = recv.at[half, mine]
@@ -250,16 +271,16 @@
         def mirror(e, carry):
             there = pl.ds(arrival(e) * devs, devs)
             for c in range(2):
-                at = pl.ds(pl.multiple_of(c * columns + start, 128), wide)
-                part[there, zone // 2, :, at] = (
-                    part[there, zone // 2, :, at] + turned_ref[c, there]
+                span = pl.ds(pl.multiple_of(c * columns + start, 128), wide)
+                part[there, zone // 2, :, span] = (
+                    part[there, zone // 2, :, span] + turned_ref[c, there]
                 )
             return carry
 
-        lax.fori_loop(0, step // 2, mirror, 0)
+        lax.fori_loop(0, at, mirror, 0)
         return carry
 
-    def send_rows(zone, slot, half=None, ready=None):
+    def send_rows(zone, slot, half=None, ready=None, first=0, last=devs):
         def one(k, carry):
             device = zone * devs + k
             if ready is not None:
@@ -282,7 +303,7 @@
 
             return carry
 
-        lax.fori_loop(0, devs, one, 0)
+        lax.fori_loop(first, last, one, 0)
 
     def add_chain(device):
         part[device] = part[device] + chain[device]
@@ -305,8 +326,8 @@
 
         @pl.when(outer)
         def _():
-            for i, zone in enumerate((far, across)):
-                mine = pl.ds(zone * devs, devs)
+            for i in range(4):
+                mine = pl.ds((far, across)[i // 2] * devs + i % 2 * chips, chips)
                 pltpu.make_async_remote_copy(
                     src_ref=part.at[mine], dst_ref=chain.at[mine], send_sem=row_send,
                     recv_sem=chain_sem.at[i], device_id=(beside * devs + 2 * chip + 1,),
@@ -317,12 +338,12 @@
 
         @pl.when(inner)
         def _():
-            for i, zone in enumerate((far, across)):
-                came = chain.at[pl.ds(zone * devs, devs)]
+            send_rows(beside, 1, 1 - near)
+            for i in range(4):
+                zone, first = (far, across)[i // 2], i % 2 * chips
+                came = chain.at[pl.ds(zone * devs + first, chips)]
                 pltpu.make_async_copy(came, came, chain_sem.at[i]).wait()
-                send_rows(zone, 2, ready=add_chain)
-                if i == 0:
-                    send_rows(beside, 1, 1 - near)
+                send_rows(zone, 2, ready=add_chain, first=first, last=first + chips)
             send_rows(plane, 0, 1 - near)
 
     def gathered(slot):
@@ -384,9 +405,11 @@
             pltpu.SemaphoreType.DMA((3,)),
             pltpu.SemaphoreType.DMA,
             pltpu.SemaphoreType.DMA((PLANES, 2)),
-            pltpu.SemaphoreType.DMA((2,)),
+            pltpu.SemaphoreType.DMA((4,)),
             pltpu.SemaphoreType.DMA,
             pltpu.SemaphoreType.DMA((3,)),
+            pltpu.SemaphoreType.REGULAR,
+            pltpu.SemaphoreType.REGULAR,
             pltpu.SemaphoreType.REGULAR,
         ],
         compiler_params=pltpu.CompilerParams(

time: 35.7 us -> 35.1 us (0.983)
  Pallas kernels: 34.3 us -> 33.7 us
    pallas_call x1, Pallas kernels: 34.3 us -> 33.7 us  [local(): pl.pallas_call(functools.partial(exchange_kernel, n, 8.0 / amps), out_sha...]
where the time goes in v5:
time: 35.1 us; the launch traced here: 34.9 us
  Pallas kernels  33.7 us (96%)
  between operations  0.64 us (2%)
  local copies, waits for them, and re-layouts  0.61 us (2%)
    pallas_call x1, Pallas kernels, local(): pl.pallas_call(functools.partial(exchange_kernel, n, 8.0 / amps), out_sha...  33.7 us

profile of v5, /device:TPU:0, one launch (start us, length us, event | category | flops | bytes accessed | tf_op | source)
XLA Modules:
  0.0 34.9 jit_solution(1831165957329351507)
XLA Ops:
  0.6 33.7 %shard_map.50 = f32[8,512]{1,0:T(8,128)S(1)} custom-call(s32[3]{0:T(128)} %sub_hbm.1, f32[128,8,128]{2,1,0:T(8,128)} %bitcast.2, f32[128,8,128]{2,1,0:T(8,128)} %bitcast.3), custom_call_target="tpu_custom_call" | custom-call | tf_op jit(solution)/shard_map/pallas_call | solution.py:384
  34.3 0.6 %fusion = (f32[8,256]{1,0:T(8,128)}, f32[8,256]{1,0:T(8,128)}) fusion(f32[8,512]{1,0:T(8,128)S(1)} %shard_map.50), kind=kLoop, calls=%fused_computation | loop fusion | bytes 32768 | tf_op jit(solution)/shard_map/slice | solution.py:419

commit v6 on v5

--- a/solution.py
+++ b/solution.py
@@ -13,7 +13,7 @@
 
 def exchange_kernel(n, scale, sub_hbm, re_hbm, im_hbm, out_ref, sub_ref, state, mixed, send, recv,
                     high_ref, low_ref, part, turned_ref, chain, rows, load_sem, send_sem,
-                    recv_sem, chain_sem, row_send, row_recv, present, outer_in, go):
+                    recv_sem, chain_sem, row_send, row_recv, present, outer_in, column_in, go):
     me = lax.axis_index("dev")
     loads = [
         pltpu.make_async_copy(sub_hbm, sub_ref, load_sem.at[2]),
@@ -42,17 +42,34 @@
     def signal(sem, device):
         pl.semaphore_signal(sem, inc=1, device_id=(device,), device_id_type=MESH)
 
+    beside_core = beside * devs + 2 * chip
+
     @pl.when(inner & (core == 1))
     def _():
         def greet(k, carry):
-            signal(barrier, jnp.bitwise_xor(me, n - k))
-            return carry
-
-        lax.fori_loop(1, n, greet, 0)
+            device = devs + k
+
+            @pl.when(device != me)
+            def _():
+                signal(barrier, device)
+
+            return carry
+
+        lax.fori_loop(0, 2 * devs, greet, 0)
+        signal(barrier, beside_core)
+        signal(barrier, beside_core + 1)
 
     @pl.when(outer | (core == 0))
     def _():
         signal(barrier, mate)
+
+    @pl.when(outer)
+    def _():
+        pl.semaphore_wait(barrier, 2)
+
+    @pl.when(outer & (core == 1))
+    def _():
+        signal(outer_in, beside_core + 1)
 
     vregs = state.shape[1]
     quarter = vregs // 4
@@ -96,21 +113,26 @@
             jnp.where(keep, b, pltpu.roll(a, back, axis)),
         )
 
-    for c in range(2):
-        loads[1 + c].wait()
-
-        def first_pass(v, carry):
-            x = [state[c, v + quarter * k] for k in range(4)]
-            x[0], x[2] = swap(x[0], x[2], high4, high4, 4, 0)
-            x[1], x[3] = swap(x[1], x[3], high4, high4, 4, 0)
-            for k in (0, 2):
-                a, b = swap(x[k], x[k + 1], odd_lane, odd_lane, 1, 1)
-                x[k], x[k + 1] = swap(a, b, odd_sub, odd_sub, 1, 0)
-            for k in range(4):
-                mixed[c, v + quarter * k] = x[k]
-            return carry
-
-        lax.fori_loop(0, quarter, first_pass, 0, unroll=32)
+    def spread(c, v):
+        x = [state[c, v + quarter * k] for k in range(4)]
+        x[0], x[2] = swap(x[0], x[2], high4, high4, 4, 0)
+        x[1], x[3] = swap(x[1], x[3], high4, high4, 4, 0)
+        for k in (0, 2):
+            a, b = swap(x[k], x[k + 1], odd_lane, odd_lane, 1, 1)
+            x[k], x[k + 1] = swap(a, b, odd_sub, odd_sub, 1, 0)
+        return x
+
+    def fresh(c, at):
+        x = spread(c, lax.rem(at, quarter))
+        for k in range(3):
+            x[3] = jnp.where(at // quarter == k, x[k], x[3])
+        return x[3]
+
+    def first_pass(v, carry):
+        for c in range(2):
+            for k, value in enumerate(spread(c, v)):
+                mixed[c, v + quarter * k] = value
+        return carry
 
     pairs = width // 2
     tiles = width // 2
@@ -118,14 +140,14 @@
     def target(zone, k):
         return zone * chips + jnp.bitwise_xor(chip, chips - 1 - k)
 
-    def pack(owner):
+    def pack(owner, read):
         for c in range(2):
             for p in range(pairs):
                 u = owner * pairs + p
                 low = jnp.bitwise_and(u, stride - 1)
                 first = 2 * u - low
-                a = mixed[c, first]
-                b = mixed[c, first + stride]
+                a = read(c, first)
+                b = read(c, first + stride)
                 a, b = swap(a, b, lane_hit, lane_keep, lane_step, 1)
                 a, b = swap(a, b, sub_hit, sub_keep, 2, 0)
                 for w, value in enumerate((a, b)):
@@ -135,7 +157,7 @@
 
     def pack_group(zone, start):
         def one(k, carry):
-            pack(target(zone, k))
+            pack(target(zone, k), lambda c, at: mixed[c, at])
             return carry
 
         lax.fori_loop(start, chips, one, 0, unroll=4 - start if chips >= 4 else 1)
@@ -165,33 +187,55 @@
 
         lax.fori_loop(0, 2 * count, one, 0)
 
-    pack(target(across, 0))
-    pl.semaphore_wait(barrier, owners // 2 + jnp.where(outer, 1, 0))
+    for load in loads[1:]:
+        load.wait()
+    pack(target(across, 0), fresh)
+    @pl.when(inner)
+    def _():
+        pl.semaphore_wait(barrier, owners // 2)
+
+    @pl.when(outer)
+    def _():
+        pl.semaphore_wait(go.at[0], 1)
 
     @pl.when(outer & (core == 1))
     def _():
+        signal(go.at[0], mate)
+
+    send_group(across, 0, 1)
+
+    @pl.when(inner & (core == 1))
+    def _():
+        pl.semaphore_wait(outer_in, 1)
+        signal(go.at[0], beside_core + 1)
+
         def tell(k, carry):
-            signal(outer_in, devs + 2 * k + 1)
+            device = devs + 2 * k + 1
+
+            @pl.when(device != me)
+            def _():
+                signal(column_in, device)
+
             return carry
 
         lax.fori_loop(0, owners // 2, tell, 0)
 
-    send_group(across, 0, 1)
+    lax.fori_loop(0, quarter, first_pass, 0, unroll=16)
     pack_group(far, 0)
 
     @pl.when(inner & (core == 1))
     def _():
-        pl.semaphore_wait(outer_in, owners // 2)
-        signal(go, mate)
-        signal(go, beside * devs + 2 * chip + 1)
+        pl.semaphore_wait(column_in, owners // 2 - 1)
+        signal(go.at[1], mate)
+        signal(go.at[1], beside_core + 1)
 
     @pl.when(outer | (core == 0))
     def _():
-        pl.semaphore_wait(go, 1)
+        pl.semaphore_wait(go.at[1], 1)
 
     @pl.when(outer & (core == 1))
     def _():
-        signal(go, mate)
+        signal(go.at[1], mate)
 
     send_group(far, 0, chips)
     pack_group(beside, 0)
@@ -338,12 +382,16 @@
 
         @pl.when(inner)
         def _():
-            send_rows(beside, 1, 1 - near)
             for i in range(4):
                 zone, first = (far, across)[i // 2], i % 2 * chips
                 came = chain.at[pl.ds(zone * devs + first, chips)]
                 pltpu.make_async_copy(came, came, chain_sem.at[i]).wait()
-                send_rows(zone, 2, ready=add_chain, first=first, last=first + chips)
+                if i == 0:
+                    pair = min(2, chips)
+                    send_rows(zone, 2, ready=add_chain, last=pair)
+                    send_rows(beside, 1, 1 - near)
+                    first = pair
+                send_rows(zone, 2, ready=add_chain, first=first, last=i % 2 * chips + chips)
             send_rows(plane, 0, 1 - near)
 
     def gathered(slot):
@@ -411,6 +459,7 @@
             pltpu.SemaphoreType.REGULAR,
             pltpu.SemaphoreType.REGULAR,
             pltpu.SemaphoreType.REGULAR,
+            pltpu.SemaphoreType.REGULAR((2,)),
         ],
         compiler_params=pltpu.CompilerParams(
             collective_id=0, has_side_effects=True, vmem_limit_bytes=56 * 2**20

time: 35.1 us -> 35 us (level)
  no operation moved by 1% of the time
where the time goes in v6:
time: 35 us; the launch traced here: 34.9 us
  Pallas kernels  33.6 us (96%)
  between operations  0.64 us (2%)
  local copies, waits for them, and re-layouts  0.61 us (2%)
    pallas_call x1, Pallas kernels, local(): pl.pallas_call(functools.partial(exchange_kernel, n, 8.0 / amps), out_sha...  33.6 us

profile of v6, /device:TPU:0, one launch (start us, length us, event | category | flops | bytes accessed | tf_op | source)
XLA Modules:
  0.0 34.9 jit_solution(373308271308887846)
XLA Ops:
  0.6 33.6 %shard_map.50 = f32[8,512]{1,0:T(8,128)S(1)} custom-call(s32[3]{0:T(128)} %sub_hbm.1, f32[128,8,128]{2,1,0:T(8,128)} %bitcast.2, f32[128,8,128]{2,1,0:T(8,128)} %bitcast.3), custom_call_target="tpu_custom_call" | custom-call | tf_op jit(solution)/shard_map/pallas_call | solution.py:432
  34.3 0.6 %fusion = (f32[8,256]{1,0:T(8,128)}, f32[8,256]{1,0:T(8,128)}) fusion(f32[8,512]{1,0:T(8,128)S(1)} %shard_map.50), kind=kLoop, calls=%fused_computation | loop fusion | bytes 32768 | tf_op jit(solution)/shard_map/slice | solution.py:468

commit v7 on v6

--- a/solution.py
+++ b/solution.py
@@ -11,8 +11,13 @@
 PLANES = 4
 
 
-def exchange_kernel(n, scale, sub_hbm, re_hbm, im_hbm, out_ref, sub_ref, state, mixed, send, recv,
-                    high_ref, low_ref, part, turned_ref, chain, rows, load_sem, send_sem,
+def piece_tiles(width):
+    last = max(1, width // 4)
+    return width - last, last
+
+
+def exchange_kernel(n, scale, sub_hbm, re_hbm, im_hbm, out_ref, sub_ref, state, mixed, send_a,
+                    send_b, recv_a, recv_b, high_a, high_b, low_a, low_b, part, turned_ref, chain, rows, load_sem, send_sem,
                     recv_sem, chain_sem, row_send, row_recv, present, outer_in, column_in, go):
     me = lax.axis_index("dev")
     loads = [
@@ -135,8 +140,9 @@
         return carry
 
     pairs = width // 2
-    tiles = width // 2
-    depth = tiles * 128
+    send, recv = (send_a, send_b), (recv_a, recv_b)
+    high_ref, low_ref = (high_a, high_b), (low_a, low_b)
+    tiles = piece_tiles(width)
     def target(zone, k):
         return zone * chips + jnp.bitwise_xor(chip, chips - 1 - k)
 
@@ -151,9 +157,10 @@
                 a, b = swap(a, b, lane_hit, lane_keep, lane_step, 1)
                 a, b = swap(a, b, sub_hit, sub_keep, 2, 0)
                 for w, value in enumerate((a, b)):
-                    half, tile = divmod(2 * p + w, tiles)
-                    column = (c * tiles + tile) * 128
-                    send[owner, half, :, column : column + 128] = value
+                    tile = 2 * p + w
+                    piece = int(tile >= tiles[0])
+                    column = (c * tiles[piece] + tile - piece * tiles[0]) * 128
+                    send[piece][owner, :, column : column + 128] = value
 
     def pack_group(zone, start):
         def one(k, carry):
@@ -163,29 +170,27 @@
         lax.fori_loop(start, chips, one, 0, unroll=4 - start if chips >= 4 else 1)
 
     def send_group(zone, start, stop):
-        count = stop - start
-
-        def one(k, carry):
-            owner = target(zone, start + lax.rem(k, count))
-            half = k // count
-            device = 2 * owner + 1
-
-            @pl.when(device != me)
-            def _():
-                pltpu.make_async_remote_copy(
-                    src_ref=send.at[owner, half], dst_ref=recv.at[half, me], send_sem=send_sem,
-                    recv_sem=recv_sem.at[plane, half], device_id=(device,), device_id_type=MESH,
-                ).start()
-
-            @pl.when(device == me)
-            def _():
-                pltpu.make_async_copy(
-                    send.at[owner, half], recv.at[half, me], recv_sem.at[plane, half]
-                ).start()
-
-            return carry
-
-        lax.fori_loop(0, 2 * count, one, 0)
+        for piece in range(2):
+            def one(k, carry):
+                owner = target(zone, k)
+                device = 2 * owner + 1
+                arrived = recv_sem.at[plane, piece]
+                source, there = send[piece].at[owner], recv[piece].at[me]
+
+                @pl.when(device != me)
+                def _():
+                    pltpu.make_async_remote_copy(
+                        src_ref=source, dst_ref=there, send_sem=send_sem, recv_sem=arrived,
+                        device_id=(device,), device_id_type=MESH,
+                    ).start()
+
+                @pl.when(device == me)
+                def _():
+                    pltpu.make_async_copy(source, there, arrived).start()
+
+                return carry
+
+            lax.fori_loop(start, stop, one, 0)
 
     for load in loads[1:]:
         load.wait()
@@ -267,6 +272,7 @@
         return lax.dot_general(x, y, (((1,), (1,)), ((), ())), preferred_element_type=jnp.float32)
 
     def stacked(x):
+        depth = x.shape[1] // 2
         return jnp.concatenate(
             [x, jnp.concatenate([x[:, depth:], -x[:, :depth]], axis=1)], axis=0
         )
@@ -279,28 +285,25 @@
             s == 0, plane, jnp.where(s == 1, second, jnp.where(s == 2, third, last))
         )
 
-    def gram(step, carry):
-        crossed = outer & (step >= 4)
-        at = jnp.where(crossed, 2 + lax.rem(step, 2), step // 2)
-        half = jnp.where(crossed, step // 2 - 2, lax.rem(step, 2))
+    def gram(at, piece):
         zone = arrival(at)
         mine = pl.ds(zone * devs, devs)
         lines = pl.ds(pl.multiple_of(zone * block, block), block)
-        came = recv.at[half, mine]
-        pltpu.make_async_copy(came, came, recv_sem.at[zone, half]).wait()
-        high, low = split(recv[half, mine].reshape(block, 2 * depth))
-        high_ref[half, lines] = high
-        low_ref[half, lines] = low
+        came = recv[piece].at[mine]
+        pltpu.make_async_copy(came, came, recv_sem.at[zone, piece]).wait()
+        high, low = split(recv[piece][mine].reshape(block, 256 * tiles[piece]))
+        high_ref[piece][lines] = high
+        low_ref[piece][lines] = low
         left_h = stacked(high)
-        both = dot(jnp.concatenate([left_h, stacked(low)], axis=0), high_ref[half])
-        result = both[: 2 * block] + (both[2 * block :] + dot(left_h, low_ref[half]))
+        both = dot(jnp.concatenate([left_h, stacked(low)], axis=0), high_ref[piece][...])
+        result = both[: 2 * block] + (both[2 * block :] + dot(left_h, low_ref[piece][...]))
         start = lax.rem(zone * block, columns) // wide * wide
         for c in range(2):
             value = result[c * block : (c + 1) * block]
             here = slice(c * columns, (c + 1) * columns)
             for side in range(2):
-                piece = value[:, side * columns : (side + 1) * columns]
-                part[mine, side, :, here] = part[mine, side, :, here] + piece.reshape(
+                added = value[:, side * columns : (side + 1) * columns]
+                part[mine, side, :, here] = part[mine, side, :, here] + added.reshape(
                     devs, 8, columns
                 )
             if c == 1:
@@ -322,7 +325,6 @@
             return carry
 
         lax.fori_loop(0, at, mirror, 0)
-        return carry
 
     def send_rows(zone, slot, half=None, ready=None, first=0, last=devs):
         def one(k, carry):
@@ -355,18 +357,25 @@
     @pl.when(core == 1)
     def _():
         pl.semaphore_wait(present, owners)
-        high_ref[...] = jnp.zeros_like(high_ref)
-        low_ref[...] = jnp.zeros_like(low_ref)
-        part[...] = jnp.zeros_like(part)
-        lax.fori_loop(0, 2 * PLANES - 2, gram, 0)
+        for ref in (*high_ref, *low_ref, part):
+            ref[...] = jnp.zeros_like(ref)
+
         near = plane // 2
 
-        @pl.when(inner)
-        def _():
-            send_rows(beside, 1, near)
-            send_rows(plane, 0, near)
-
-        lax.fori_loop(2 * PLANES - 2, 2 * PLANES, gram, 0)
+        def step(i, carry):
+            crossed = outer & (i >= 4)
+            at = jnp.where(crossed, 2 + lax.rem(i, 2), i // 2)
+            piece = jnp.where(crossed, i // 2 - 2, lax.rem(i, 2))
+            for p in range(2):
+                pl.when(piece == p)(functools.partial(gram, at, p))
+
+            @pl.when(inner & ((i == 5) | (i == 7)))
+            def _():
+                send_rows(beside, 1, jnp.where(i == 5, near, 1 - near))
+
+            return carry
+
+        lax.fori_loop(0, 2 * PLANES, step, 0)
 
         @pl.when(outer)
         def _():
@@ -382,17 +391,15 @@
 
         @pl.when(inner)
         def _():
-            for i in range(4):
-                zone, first = (far, across)[i // 2], i % 2 * chips
+            def relay(i, carry):
+                zone, first = jnp.where(i < 2, far, across), lax.rem(i, 2) * chips
                 came = chain.at[pl.ds(zone * devs + first, chips)]
                 pltpu.make_async_copy(came, came, chain_sem.at[i]).wait()
-                if i == 0:
-                    pair = min(2, chips)
-                    send_rows(zone, 2, ready=add_chain, last=pair)
-                    send_rows(beside, 1, 1 - near)
-                    first = pair
-                send_rows(zone, 2, ready=add_chain, first=first, last=i % 2 * chips + chips)
-            send_rows(plane, 0, 1 - near)
+                send_rows(zone, 2, ready=add_chain, first=first, last=first + chips)
+                return carry
+
+            lax.fori_loop(0, 4, relay, 0)
+            send_rows(plane, 0)
 
     def gathered(slot):
         pltpu.make_async_copy(rows.at[slot], rows.at[slot], row_recv.at[slot]).wait()
@@ -407,12 +414,14 @@
             at = c * full + side * columns
             out_ref[:, at : at + columns] = total[side, :, c * columns : (c + 1) * columns]
 
-    rest = send.at[pl.ds(0, owners - 1)]
-    pltpu.make_async_copy(rest, rest, send_sem).wait()
+    for ref in send:
+        rest = ref.at[pl.ds(0, owners - 1)]
+        pltpu.make_async_copy(rest, rest, send_sem).wait()
 
     @pl.when(core == 0)
     def _():
-        pltpu.make_async_copy(send.at[0], send.at[0], send_sem).wait()
+        for ref in send:
+            pltpu.make_async_copy(ref.at[0], ref.at[0], send_sem).wait()
 
     @pl.when(core == 1)
     def _():
@@ -428,7 +437,7 @@
     full = 8 * n
     devs = n // PLANES
     wide = max(8 * devs, 128)
-    chunk = (8, width * 128)
+    depths = [256 * tiles for tiles in piece_tiles(width)]
     out = pl.pallas_call(
         functools.partial(exchange_kernel, n, 8.0 / amps),
         out_shape=pltpu.VMEM((8, 2 * full), jnp.float32),
@@ -442,10 +451,10 @@
             pltpu.SMEM((3,), jnp.int32),
             pltpu.VMEM((2, vregs, 8, 128), jnp.float32),
             pltpu.VMEM((2, vregs, 8, 128), jnp.float32),
-            pltpu.VMEM((owners, 2) + chunk, jnp.float32),
-            pltpu.VMEM((2, n) + chunk, jnp.float32),
-            pltpu.VMEM((2, full, chunk[1]), jnp.bfloat16),
-            pltpu.VMEM((2, full, chunk[1]), jnp.bfloat16),
+            *[pltpu.VMEM((owners, 8, depth), jnp.float32) for depth in depths],
+            *[pltpu.VMEM((n, 8, depth), jnp.float32) for depth in depths],
+            *[pltpu.VMEM((full, depth), jnp.bfloat16) for depth in depths],
+            *[pltpu.VMEM((full, depth), jnp.bfloat16) for depth in depths],
             pltpu.VMEM((n, 2, 8, full), jnp.float32),
             pltpu.VMEM((2, n, 8, wide), jnp.float32),
             pltpu.VMEM((n, 2, 8, full), jnp.float32),

time: 35 us -> 35 us (level)
  no operation moved by 1% of the time
where the time goes in v7:
time: 35 us; the launch traced here: 34.8 us
  Pallas kernels  33.6 us (96%)
  between operations  0.64 us (2%)
  local copies, waits for them, and re-layouts  0.61 us (2%)
    pallas_call x1, Pallas kernels, local(): pl.pallas_call(functools.partial(exchange_kernel, n, 8.0 / amps), out_sha...  33.6 us

profile of v7, /device:TPU:0, one launch (start us, length us, event | category | flops | bytes accessed | tf_op | source)
XLA Modules:
  0.0 34.8 jit_solution(1139346086132162602)
XLA Ops:
  0.6 33.6 %shard_map.50 = f32[8,512]{1,0:T(8,128)S(1)} custom-call(s32[3]{0:T(128)} %sub_hbm.1, f32[128,8,128]{2,1,0:T(8,128)} %bitcast.2, f32[128,8,128]{2,1,0:T(8,128)} %bitcast.3), custom_call_target="tpu_custom_call" | custom-call | tf_op jit(solution)/shard_map/pallas_call | solution.py:441
  34.2 0.6 %fusion = (f32[8,256]{1,0:T(8,128)}, f32[8,256]{1,0:T(8,128)}) fusion(f32[8,512]{1,0:T(8,128)S(1)} %shard_map.50), kind=kLoop, calls=%fused_computation | loop fusion | bytes 32768 | tf_op jit(solution)/shard_map/slice | solution.py:477

commit v8 on v7

--- a/solution.py
+++ b/solution.py
@@ -401,32 +401,32 @@
             lax.fori_loop(0, 4, relay, 0)
             send_rows(plane, 0)
 
-    def gathered(slot):
-        pltpu.make_async_copy(rows.at[slot], rows.at[slot], row_recv.at[slot]).wait()
-        total = rows[slot, 0]
-        for k in range(1, chips):
+    for ref in send:
+        rest = ref.at[pl.ds(0, owners - 1)]
+        pltpu.make_async_copy(rest, rest, send_sem).wait()
+
+    @pl.when(core == 0)
+    def _():
+        for ref in send:
+            pltpu.make_async_copy(ref.at[0], ref.at[0], send_sem).wait()
+
+    @pl.when(core == 1)
+    def _():
+        sent = part.at[pl.ds(0, n - 1)]
+        pltpu.make_async_copy(sent, sent, row_send).wait()
+
+    def gather(slot, total):
+        came = rows.at[slot]
+        pltpu.make_async_copy(came, came, row_recv.at[slot]).wait()
+        for k in range(chips):
             total = total + rows[slot, k]
         return total
 
-    total = (gathered(0) + gathered(1) + gathered(2)) * scale
+    total = lax.fori_loop(0, 3, gather, jnp.zeros((2, 8, full), jnp.float32)) * scale
     for side in range(2):
         for c in range(2):
             at = c * full + side * columns
             out_ref[:, at : at + columns] = total[side, :, c * columns : (c + 1) * columns]
-
-    for ref in send:
-        rest = ref.at[pl.ds(0, owners - 1)]
-        pltpu.make_async_copy(rest, rest, send_sem).wait()
-
-    @pl.when(core == 0)
-    def _():
-        for ref in send:
-            pltpu.make_async_copy(ref.at[0], ref.at[0], send_sem).wait()
-
-    @pl.when(core == 1)
-    def _():
-        sent = part.at[pl.ds(0, n - 1)]
-        pltpu.make_async_copy(sent, sent, row_send).wait()
 
 
 def local(n, state_real, state_imag, subsystem):

time: 35 us -> 35 us (level)
  no operation moved by 1% of the time
where the time goes in v8:
time: 35 us; the launch traced here: 34.8 us
  Pallas kernels  33.6 us (96%)
  between operations  0.64 us (2%)
  local copies, waits for them, and re-layouts  0.61 us (2%)
    pallas_call x1, Pallas kernels, local(): pl.pallas_call(functools.partial(exchange_kernel, n, 8.0 / amps), out_sha...  33.6 us

profile of v8, /device:TPU:0, one launch (start us, length us, event | category | flops | bytes accessed | tf_op | source)
XLA Modules:
  0.0 34.8 jit_solution(10617184749173508946)
XLA Ops:
  0.6 33.6 %shard_map.50 = f32[8,512]{1,0:T(8,128)S(1)} custom-call(s32[3]{0:T(128)} %sub_hbm.1, f32[128,8,128]{2,1,0:T(8,128)} %bitcast.2, f32[128,8,128]{2,1,0:T(8,128)} %bitcast.3), custom_call_target="tpu_custom_call" | custom-call | tf_op jit(solution)/shard_map/pallas_call | solution.py:441
  34.2 0.6 %fusion = (f32[8,256]{1,0:T(8,128)}, f32[8,256]{1,0:T(8,128)}) fusion(f32[8,512]{1,0:T(8,128)S(1)} %shard_map.50), kind=kLoop, calls=%fused_computation | loop fusion | bytes 32768 | tf_op jit(solution)/shard_map/slice | solution.py:477

commit v9 on v8

--- a/solution.py
+++ b/solution.py
@@ -369,9 +369,9 @@
             for p in range(2):
                 pl.when(piece == p)(functools.partial(gram, at, p))
 
-            @pl.when(inner & ((i == 5) | (i == 7)))
+            @pl.when(inner & ((i == 4) | (i == 7)))
             def _():
-                send_rows(beside, 1, jnp.where(i == 5, near, 1 - near))
+                send_rows(beside, 1, jnp.where(i == 4, near, 1 - near))
 
             return carry
 

time: 35 us -> 35 us (level)
  no operation moved by 1% of the time
where the time goes in v9:
time: 35 us; the launch traced here: 34.8 us
  Pallas kernels  33.6 us (96%)
  between operations  0.64 us (2%)
  local copies, waits for them, and re-layouts  0.61 us (2%)
    pallas_call x1, Pallas kernels, local(): pl.pallas_call(functools.partial(exchange_kernel, n, 8.0 / amps), out_sha...  33.6 us

profile of v9, /device:TPU:0, one launch (start us, length us, event | category | flops | bytes accessed | tf_op | source)
XLA Modules:
  0.0 34.8 jit_solution(7905243055952779069)
XLA Ops:
  0.6 33.6 %shard_map.50 = f32[8,512]{1,0:T(8,128)S(1)} custom-call(s32[3]{0:T(128)} %sub_hbm.1, f32[128,8,128]{2,1,0:T(8,128)} %bitcast.2, f32[128,8,128]{2,1,0:T(8,128)} %bitcast.3), custom_call_target="tpu_custom_call" | custom-call | tf_op jit(solution)/shard_map/pallas_call | solution.py:441
  34.2 0.6 %fusion = (f32[8,256]{1,0:T(8,128)}, f32[8,256]{1,0:T(8,128)}) fusion(f32[8,512]{1,0:T(8,128)S(1)} %shard_map.50), kind=kLoop, calls=%fused_computation | loop fusion | bytes 32768 | tf_op jit(solution)/shard_map/slice | solution.py:477

commit v10 on v9

--- a/solution.py
+++ b/solution.py
@@ -369,9 +369,9 @@
             for p in range(2):
                 pl.when(piece == p)(functools.partial(gram, at, p))
 
-            @pl.when(inner & ((i == 4) | (i == 7)))
+            @pl.when(inner & ((i == 3) | (i == 7)))
             def _():
-                send_rows(beside, 1, jnp.where(i == 4, near, 1 - near))
+                send_rows(beside, 1, jnp.where(i == 3, near, 1 - near))
 
             return carry
 

time: 35 us -> 35 us (level)
  no operation moved by 1% of the time
where the time goes in v10:
time: 35 us; the launch traced here: 34.8 us
  Pallas kernels  33.6 us (96%)
  between operations  0.64 us (2%)
  local copies, waits for them, and re-layouts  0.61 us (2%)
    pallas_call x1, Pallas kernels, local(): pl.pallas_call(functools.partial(exchange_kernel, n, 8.0 / amps), out_sha...  33.6 us

profile of v10, /device:TPU:0, one launch (start us, length us, event | category | flops | bytes accessed | tf_op | source)
XLA Modules:
  0.0 34.8 jit_solution(11354486843175410778)
XLA Ops:
  0.6 33.6 %shard_map.50 = f32[8,512]{1,0:T(8,128)S(1)} custom-call(s32[3]{0:T(128)} %sub_hbm.1, f32[128,8,128]{2,1,0:T(8,128)} %bitcast.2, f32[128,8,128]{2,1,0:T(8,128)} %bitcast.3), custom_call_target="tpu_custom_call" | custom-call | tf_op jit(solution)/shard_map/pallas_call | solution.py:441
  34.2 0.6 %fusion = (f32[8,256]{1,0:T(8,128)}, f32[8,256]{1,0:T(8,128)}) fusion(f32[8,512]{1,0:T(8,128)S(1)} %shard_map.50), kind=kLoop, calls=%fused_computation | loop fusion | bytes 32768 | tf_op jit(solution)/shard_map/slice | solution.py:477
